TPU v7x, 32 devices: a whole 2x2x4 slice. The times are simulated.
32 devices in a mesh: seq: 8 (over z, x), head: 4 (over y, core).
Axes of the slice: x: 2, y: 2, z: 4, core: 2. Of those that a mesh axis runs over, the one named last changes fastest.
Arguments:
- tokens: bfloat16 [8192, 1024], P(('seq', 'head')), may hold values from -6 to 6
- seq_lengths: int32 [8, 1], P('seq'), may hold values from 1024 to 1024, as said below
- w_qkvu: bfloat16 [4, 1024, 1024], replicated, may hold values from -0.1875 to 0.1875
- w_out: bfloat16 [1024, 1024], replicated, may hold values from -0.1875 to 0.1875
- w_glu: bfloat16 [2, 1024, 2816], replicated, may hold values from -0.1875 to 0.1875
- w_down: bfloat16 [2816, 1024], replicated, may hold values from -0.109375 to 0.109375
- cotangent: bfloat16 [8192, 1024], P(('seq', 'head')), may hold values from -6 to 6
Outputs:
- layer_out: bfloat16 [8192, 1024], P(('seq', 'head'))
- grad_tokens: float32 [8192, 1024], P(('seq', 'head'))
- grad_qkvu: float32 [4, 1024, 1024], P(None, None, 'head')
- grad_out: float32 [1024, 1024], P('head')
- grad_glu: float32 [2, 1024, 2816], P(None, None, 'head')
- grad_down: float32 [2816, 1024], P('head')
Inputs may be any that keep to these rules, and one draw needn't show every extreme that they name: `seq_lengths`: row g lists the lengths in tokens of group g's sequences in order, each a multiple of 1024, summing to 1024, with zeros after the last. In every draw one group holds a single sequence and another holds 1 sequence of 1024 tokens.
All inputs are finite; a program needn't handle non-finite values.
Results may differ from a plain program's by a relative error of at most 0.013.
Values may be sent and summed in bfloat16 or wider, within the bound.
A program may use at most 192 MiB of HBM per device.

v0:
```python
import functools

import jax
import jax.numpy as jnp
from jax import lax
from jax.experimental import pallas as pl
from jax.experimental.pallas import tpu as pltpu
from jax.sharding import PartitionSpec as P

D = 1024
HEADS = 8
HEAD_DIM = 128
EPSILON = 1e-06
PARTS = 4
LOCAL = D // PARTS
BF = jnp.bfloat16
F32 = jnp.float32
MESH = pl.DeviceIdType.MESH


def dot(a, b):
    return lax.dot_general(a, b, (((1,), (0,)), ((), ())), preferred_element_type=F32)


def dot_nt(a, b):
    return lax.dot_general(a, b, (((1,), (1,)), ((), ())), preferred_element_type=F32)


def dot_tn(a, b):
    return lax.dot_general(a, b, (((0,), (0,)), ((), ())), preferred_element_type=F32)


def sigmoid(v):
    return 1.0 / (1.0 + jnp.exp(-v))


def rms_scale(v):
    return lax.rsqrt(jnp.mean(v * v, axis=-1, keepdims=True) + EPSILON)


def norm_back(v, scale, grad):
    normed = v * scale
    return scale * (grad - normed * jnp.mean(grad * normed, axis=-1, keepdims=True))


def round_up(n, m):
    return -(-n // m) * m


def rows(start, size, align):
    return pl.ds(pl.multiple_of(start, align), size)


class Sizes:
    def __init__(self, seq, block, ff):
        self.seq = seq
        self.tb = block
        self.t = block * PARTS
        self.fs = ff // PARTS
        self.fp = round_up(self.fs, 256)
        self.full_tiles = self.fs // 128
        self.glu_tiles = 2 * self.full_tiles + (1 if self.fs % 128 else 0)
        rest = (D // 128) * LOCAL + 4 * (LOCAL // 128) * D
        chunk = lambda n: round_up(-(-n // (2 * seq)), 16)
        self.chunk = [chunk((D // 128) * self.fs), chunk(self.glu_tiles * D), chunk(rest // 2)]
        self.chunk.append(chunk(rest - 2 * seq * self.chunk[2]))
        self.base = [2 * seq * sum(self.chunk[:i]) for i in range(5)]
        self.total = self.base[4]


class Gather:
    def __init__(self, ctx, count, own, place, first):
        self.ctx, self.count, self.own, self.place, self.first = ctx, count, own, place, first

    def copy(self, src, dst, index, target):
        c = self.ctx
        return pltpu.make_async_remote_copy(
            src_ref=src,
            dst_ref=dst,
            send_sem=c.gsend.at[index],
            recv_sem=c.grecv.at[index],
            device_id=(c.s, target),
            device_id_type=MESH,
        )

    def across(self, k):
        c = self.ctx
        return self.copy(self.own(k), self.place(c.h, k), self.first + 3 * k, c.yp)

    def beside(self, k):
        c = self.ctx
        return self.copy(self.own(k), self.place(c.h, k), self.first + 3 * k + 1, c.sib)

    def relay(self, k):
        c = self.ctx
        spot = self.place(c.yp, k)
        return self.copy(spot, spot, self.first + 3 * k + 2, c.sib)

    def start(self, k):
        self.across(k).start()
        self.beside(k).start()

    def pass_on(self, k):
        self.across(k).wait_recv()
        self.relay(k).start()

    def wait_beside(self, k):
        self.beside(k).wait_recv()

    def wait_relay(self, k):
        self.relay(k).wait_recv()

    def drain(self):
        for k in range(self.count):
            self.across(k).wait_send()
            self.beside(k).wait_send()
            self.relay(k).wait_send()


class Scatter:
    def __init__(self, ctx, part, near, cross, first):
        self.ctx, self.part, self.near, self.cross, self.first = ctx, part, near, cross, first
        self.tb = ctx.sz.tb

    def block(self, index):
        return self.part.at[rows(index * self.tb, self.tb, self.tb), :]

    def copy(self, src, dst, index, target):
        c = self.ctx
        return pltpu.make_async_remote_copy(
            src_ref=src,
            dst_ref=dst,
            send_sem=c.gsend.at[index],
            recv_sem=c.grecv.at[index],
            device_id=(c.s, target),
            device_id_type=MESH,
        )

    def beside(self, k):
        c = self.ctx
        return self.copy(self.block(2 * k + 1 - c.c), self.near.at[k], self.first + k, c.sib)

    def across(self):
        c = self.ctx
        return self.copy(self.block(c.yp), self.cross, self.first + 2, c.yp)

    def start(self):
        self.beside(0).start()
        self.beside(1).start()

    def middle(self):
        c = self.ctx
        self.beside(0).wait_recv()
        self.beside(1).wait_recv()
        there = self.block(c.yp)
        there[...] = (there[...].astype(F32) + self.near[1 - c.y].astype(F32)).astype(BF)
        self.across().start()

    def result(self, lo, size):
        c = self.ctx
        here = self.part[rows(c.h * self.tb + lo, size, size), :].astype(F32)
        at = pl.ds(lo, size)
        return here + self.near[c.y, at, :].astype(F32) + self.cross[at, :].astype(F32)

    def wait(self):
        self.across().wait_recv()

    def drain(self):
        self.beside(0).wait_send()
        self.beside(1).wait_send()
        self.across().wait_send()


class Ring:
    def __init__(self, ctx, index, slots):
        self.ctx, self.index, self.slots = ctx, index, slots
        self.base, self.chunk = ctx.sz.base[index], ctx.sz.chunk[index]
        self.n = ctx.sz.seq

    def mine(self, d, k):
        k = lax.rem(k, self.n)
        return rows(self.base + (2 * k + d) * self.chunk, self.chunk, 16)

    def copy(self, d, src, dst, step):
        c = self.ctx
        return pltpu.make_async_remote_copy(
            src_ref=src,
            dst_ref=dst,
            send_sem=c.rsend.at[self.index, d, step],
            recv_sem=c.rrecv.at[self.index, d, step],
            device_id=(c.right if d == 0 else c.left, c.h),
            device_id_type=MESH,
        )

    def toward(self, d, t):
        return self.ctx.p + (self.n - t if d == 0 else t)

    def publish(self, d, k, j):
        if self.n > 16:
            return
        at = self.mine(d, k)
        c = self.ctx
        copy = pltpu.make_async_copy(c.f.at[at, :], c.f_out.at[at, :], c.psem.at[self.index, d, j])
        copy.start()
        c.outs.append(copy)

    def reduce_copy(self, d, t, first=False):
        f = self.ctx.f
        src = f.at[self.mine(d, self.toward(d, t)), :] if first else self.slots.at[d, t - 1]
        return self.copy(d, src, self.slots.at[d, t], t)

    def reduce_send(self, t, first=False):
        for d in range(2):
            self.reduce_copy(d, t, first).start()

    def reduce_take(self, t, last=False):
        f = self.ctx.f
        pieces = 4 if self.chunk % 64 == 0 else (2 if self.chunk % 32 == 0 else 1)
        size = self.chunk // pieces
        for d in range(2):
            self.reduce_copy(d, t, first=True).wait_recv()
            k = lax.rem(self.toward(d, t) + (self.n - 1 if d == 0 else 1), self.n)
            start = self.base + (2 * k + d) * self.chunk
            for i in range(pieces):
                at = rows(start + i * size, size, 16)
                inside = pl.ds(i * size, size)
                total = f[at, :].astype(F32) + self.slots[d, t, inside, :].astype(F32)
                if last:
                    f[at, :] = total.astype(BF)
                else:
                    self.slots[d, t, inside, :] = total.astype(BF)
            if last:
                self.publish(d, k, self.n - 1)

    def spread_copy(self, d, t):
        spot = self.ctx.f.at[self.mine(d, self.toward(d, t) + (1 if d == 0 else self.n - 1)), :]
        return self.copy(d, spot, spot, self.n - 1 + t)

    def spread_send(self, t):
        for d in range(2):
            self.spread_copy(d, t).start()

    def spread_take(self, t):
        for d in range(2):
            self.spread_copy(d, t).wait_recv()
            if isinstance(t, int):
                self.publish(d, self.toward(d, t), t)

    def leave(self):
        for d in range(2):
            self.reduce_copy(d, 0, first=True).wait_send()

    def step(self, t):
        last = self.n - 2
        if t <= last:
            self.reduce_take(t, last=t == last)
            if t == 0:
                self.leave()
            if t < last:
                self.reduce_send(t + 1)
            else:
                self.spread_send(0)
        else:
            t -= self.n - 1
            self.spread_take(t)
            if t < last:
                self.spread_send(t + 1)

    def all_steps(self):
        last = self.n - 2

        def turn(t, carry):
            self.reduce_take(t)
            self.reduce_send(t + 1)
            return carry

        self.leave()
        lax.fori_loop(0, last, turn, 0)
        self.reduce_take(last, last=True)
        self.spread_send(0)

        def pass_on(t, carry):
            self.spread_take(t)
            self.spread_send(t + 1)
            return carry

        lax.fori_loop(0, last, pass_on, 0)
        self.spread_take(last)

    def drain(self):
        if self.n > 16:

            def one(t, carry):
                for d in range(2):
                    self.reduce_copy(d, t + 1, first=True).wait_send()
                    self.spread_copy(d, t).wait_send()
                return carry

            lax.fori_loop(0, self.n - 2, one, 0)
        else:
            for t in range(1, self.n - 1):
                for d in range(2):
                    self.reduce_copy(d, t, first=True).wait_send()
                    self.spread_copy(d, t - 1).wait_send()
        for d in range(2):
            self.spread_copy(d, self.n - 2).wait_send()


class Ctx:
    pass


def layer_kernel(sz, names, *refs):
    r = dict(zip(names, refs))
    ctx = Ctx()
    ctx.sz = sz
    seq, tb, t_all, fs, fp = sz.seq, sz.tb, sz.t, sz.fs, sz.fp
    half = seq // 2
    s, h = lax.axis_index("seq"), lax.axis_index("head")
    c, y = lax.rem(h, 2), h // 2
    z, x = s // 2, lax.rem(s, 2)
    pos = (1 - x) * z + x * (2 * half - 1 - z)

    def at_pos(p):
        q = p // half
        return (1 - q) * 2 * p + q * (2 * (2 * half - 1 - p) + 1)

    ctx.s, ctx.h, ctx.c, ctx.y, ctx.p = s, h, c, y, pos
    ctx.sib, ctx.yp = y * 2 + (1 - c), (1 - y) * 2 + c
    far = (1 - y) * 2 + (1 - c)
    ctx.right = at_pos(lax.rem(pos + 1, seq))
    ctx.left = at_pos(lax.rem(pos + seq - 1, seq))
    ctx.gsend, ctx.grecv = r["gsend"], r["grecv"]
    ctx.rsend, ctx.rrecv = r["rsend"], r["rrecv"]
    f = ctx.f = r["f"]
    ctx.f_out, ctx.psem, ctx.outs = r["f_out"], r["psem"], []
    lsem = r["lsem"]

    tok, cot, tok_g, cot_g = r["tok"], r["cot"], r["tok_g"], r["cot_g"]
    att, gate, mixed = r["att"], r["gate"], r["mixed"]

    loads = []

    def load(src, dst):
        copy = pltpu.make_async_copy(src, dst, lsem.at[len(loads)])
        copy.start()
        loads.append(copy)
        return copy

    mine = pl.ds(pl.multiple_of(h * LOCAL, LOCAL), LOCAL)
    own_rows = rows(h * tb, tb, tb)
    tok_in = load(tok, tok_g.at[own_rows, :])
    qkv_in = [
        load(r["w_qkvu"].at[k, :, mine], r["wqkv"].at[:, pl.ds(k * LOCAL, LOCAL)]) for k in range(3)
    ]
    gate_in = load(r["w_qkvu"].at[3], r["wgate"])
    out_in = load(r["w_out"], r["wout"])
    down_in = load(r["w_down"].at[rows(h * fs, fs, 64), :], r["wdown"].at[pl.ds(0, fs), :])
    glu_in = []
    window = y * (2 * fs) + c * (fs - fs % 128)
    tiles = fp // 128
    for k in range(2):
        for j in range(tiles):
            lane = pl.ds(pl.multiple_of(window + j * 128, 128), 128)
            glu_in.append(
                load(r["w_glu"].at[k, :, lane], f.at[pl.ds((k * tiles + j) * D, D), :])
            )
    cot_in = load(cot, cot_g.at[own_rows, :])

    barrier = pltpu.get_barrier_semaphore()
    for peer in ((s, ctx.sib), (s, ctx.yp), (ctx.right, h), (ctx.left, h)):
        pl.semaphore_signal(barrier, inc=1, device_id=peer, device_id_type=MESH)
    pl.semaphore_wait(barrier, 4)

    hb = tb // 2
    token_ag = Gather(
        ctx,
        2,
        lambda k: tok.at[pl.ds(k * hb, hb), :],
        lambda b, k: tok_g.at[rows(b * tb + k * hb, hb, hb), :],
        0,
    )
    cot_ag = Gather(
        ctx,
        2,
        lambda k: cot.at[pl.ds(k * hb, hb), :],
        lambda b, k: cot_g.at[rows(b * tb + k * hb, hb, hb), :],
        6,
    )
    blocks = t_all // 256
    att_place = lambda b, k: att.at[b, pl.ds(k * 256, 256), :]
    att_ag = Gather(ctx, blocks, lambda k: att_place(h, k), att_place, 33)
    low_place = lambda b, k: cot_g.at[rows(b * tb + k * hb, hb, hb), :]
    low_ag = Gather(ctx, 2, lambda k: low_place(h, k), low_place, 18)

    for k in range(2):
        token_ag.start(k)

    lane = lax.broadcasted_iota(jnp.int32, (32, HEAD_DIM), 1).astype(F32)
    step = lax.broadcasted_iota(jnp.int32, (32, HEAD_DIM), 0).astype(F32)
    frequency = jnp.exp(lane * (-9.210340371976184 / HEAD_DIM))
    fine = step * frequency
    coarse = (step * 32.0) * frequency
    cos_a, sin_a, cos_b, sin_b = jnp.cos(coarse), jnp.sin(coarse), jnp.cos(fine), jnp.sin(fine)
    for a in range(t_all // 32):
        at = pl.ds(a * 32, 32)
        ca, sa = cos_a[a : a + 1], sin_a[a : a + 1]
        r["cosine"][at, :] = ca * cos_b - sa * sin_b
        r["sine"][at, :] = sa * cos_b + ca * sin_b

    gap = lax.broadcasted_iota(jnp.int32, (256, 256), 0) - lax.broadcasted_iota(
        jnp.int32, (256, 256), 1
    )
    for e in range(2):
        slope = jnp.float32(0)
        for g in range(HEADS):
            slope = jnp.where(h * 2 + e == g, 2.0 ** (-8.0 * (g + 1) / HEADS), slope)
        for k in range(blocks):
            distance = gap + 256 * k
            value = jnp.exp(jnp.maximum(distance, 0).astype(F32) * -slope)
            r["decay"][e, k] = jnp.where(distance >= 0, value, 0.0)

    r["wdown"][pl.ds(fs, fp - fs), :] = jnp.zeros((fp - fs, D), BF)
    for one in glu_in:
        one.wait()
    part = fs % 128
    low_lanes = lax.broadcasted_iota(jnp.int32, (256, 128), 1) < 128 - part
    keep = lax.broadcasted_iota(jnp.int32, (256, 128), 1) < part if part else None

    def window_rows(n, carry):
        k, i = n // (D // 256), lax.rem(n, D // 256)
        first = k * tiles * D + i * 256
        tile = [f[rows(first + j * D, 256, 256), :].astype(F32) for j in range(tiles)]
        for j in range(tiles):
            value = tile[j]
            if part:
                straight = jnp.where(keep, value, 0.0) if j == tiles - 1 else value
                after = pltpu.roll(tile[j + 1], 128 - part, 1) if j < tiles - 1 else 0.0
                moved = jnp.where(low_lanes, pltpu.roll(value, 128 - part, 1), after)
                value = jnp.where(c == 1, moved, straight)
            lanes = pl.ds(pl.multiple_of(k * fp + j * 128, 128), 128)
            r["wglu"][rows(i * 256, 256, 256), lanes] = value.astype(BF)
        return carry

    lax.fori_loop(0, 2 * (D // 256), window_rows, 0)

    tok_in.wait()
    for one in qkv_in:
        one.wait()
    gate_in.wait()

    def project(b):
        at = rows(b * tb, tb, tb)
        v = tok_g[at, :].astype(F32)
        n1 = (v * rms_scale(v)).astype(BF)
        r["n1"][at, :] = n1
        qkv = dot(n1, r["wqkv"][...]).astype(BF)
        r["raw"][at, :] = qkv
        co, si = r["cosine"][at, :], r["sine"][at, :]
        for e in range(2):
            for name, first in (("qpos", 0), ("kpos", LOCAL)):
                w = qkv[:, first + e * HEAD_DIM : first + (e + 1) * HEAD_DIM].astype(F32)
                act = w * sigmoid(w)
                r[name][e, at, pl.ds(0, HEAD_DIM)] = (act * co).astype(BF)
                r[name][e, at, pl.ds(HEAD_DIM, HEAD_DIM)] = (act * si).astype(BF)
        for k in range(PARTS):
            gate[k, at, :] = dot(n1, r["wgate"][:, pl.ds(k * LOCAL, LOCAL)]).astype(BF)

    def project_turn(k, carry):
        @pl.when(k == 1)
        def _():
            for i in range(2):
                token_ag.wait_beside(i)

        @pl.when(k == 2)
        def _():
            for i in range(2):
                token_ag.pass_on(i)
            for i in range(2):
                cot_ag.start(i)

        @pl.when(k == 3)
        def _():
            for i in range(2):
                token_ag.wait_relay(i)

        yy = y + (k // 2) * (1 - 2 * y)
        cc = c + lax.rem(k, 2) * (1 - 2 * c)
        project(yy * 2 + cc)
        return carry

    lax.fori_loop(0, PARTS, project_turn, 0)

    value_at = 2 * LOCAL

    def attend(i):
        at = pl.ds(i * 256, 256)

        def one_head(e, carry):
            lanes = rows(value_at + e * HEAD_DIM, HEAD_DIM, HEAD_DIM)
            q = r["qpos"][e, at, :]
            total = jnp.zeros((256, HEAD_DIM), F32)
            for j in range(i + 1):
                near = pl.ds(j * 256, 256)
                scores = (dot_nt(q, r["kpos"][e, near, :]) * r["decay"][e, i - j]).astype(BF)
                r["scores"][e, at, near] = scores
                total += dot(scores, r["raw"][near, lanes])
            att[h, at, rows(e * HEAD_DIM, HEAD_DIM, HEAD_DIM)] = total.astype(BF)
            return carry

        lax.fori_loop(0, 2, one_head, 0)

    for i in range(blocks):
        attend(i)
        att_ag.start(i)

    out_in.wait()
    down_in.wait()
    cot_in.wait()
    cot_ag.pass_on(0)
    cot_ag.pass_on(1)
    for k in range(2):
        cot_ag.wait_beside(k)
        cot_ag.wait_relay(k)

    def mlp(b, carry):
        for k in range(blocks):

            @pl.when(b == k)
            def _():
                att_ag.pass_on(k)
                att_ag.wait_beside(k)
                att_ag.wait_relay(k)

        at = rows(b * 256, 256, 256)
        a = [att[k, at, :].astype(F32) for k in range(PARTS)]
        ssq = sum(jnp.sum(v * v, axis=-1, keepdims=True) for v in a)
        scale = lax.rsqrt(ssq * (1.0 / D) + EPSILON)
        hidden = tok_g[at, :].astype(F32)
        for k in range(PARTS):
            g = gate[k, at, :].astype(F32)
            m = (a[k] * scale * (g * sigmoid(g))).astype(BF)
            mixed[k, at, :] = m
            hidden += dot(m, r["wout"][pl.ds(k * LOCAL, LOCAL), :])

        @pl.when(b == h)
        def _():
            r["hidden"][...] = hidden

        n2 = (hidden * rms_scale(hidden)).astype(BF)
        r["n2"][at, :] = n2
        g = dot(n2, r["wglu"][:, pl.ds(0, fp)])
        u = dot(n2, r["wglu"][:, pl.ds(fp, fp)])
        product = (g * u).astype(BF)
        r["product"][at, :] = product
        dp = dot_nt(cot_g[at, :], r["wdown"][...])
        dg = (dp * u).astype(BF)
        du = (dp * g).astype(BF)
        r["dpair"][at, pl.ds(0, fp)] = dg
        r["dpair"][at, pl.ds(fp, fp)] = du
        return carry

    def partials(b, carry):
        at = rows(b * 256, 256, 256)
        r["lo_part"][at, :] = dot(r["product"][at, :], r["wdown"][...]).astype(BF)
        r["dn_part"][at, :] = dot_nt(r["dpair"][at, :], r["wglu"][...]).astype(BF)
        return carry

    token_ag.drain()
    lax.fori_loop(0, blocks, mlp, 0)

    dn_rs = Scatter(ctx, r["dn_part"], r["dn_near"], r["dn_cross"], 24)
    lo_rs = Scatter(ctx, r["lo_part"], r["lo_near"], r["lo_cross"], 27)
    one_rs = Scatter(ctx, r["lo_part"], r["one_near"], r["one_cross"], 30)
    rings = [Ring(ctx, i, r["slots%d" % i]) for i in range(4)]

    base = sz.base[0]
    for j in range(fp // 256):
        size = min(256, fs - j * 256)
        g = dot_tn(r["product"][:, pl.ds(j * 256, 256)], cot_g[...]).astype(BF)
        for k in range(D // 128):
            f[pl.ds(base + k * fs + j * 256, size), :] = g[:size, k * 128 : (k + 1) * 128]
    rings[0].reduce_send(0, first=True)

    base_g = sz.base[1]
    full = sz.full_tiles

    def glu_grad(j, carry):
        g = dot_tn(r["n2"][:, rows(j * 256, 256, 256)], r["dpair"][...])
        for k in range(2):
            for i in range(full):
                at = rows(base_g + (k * full + i) * D + j * 256, 256, 16)
                first = k * fp + i * 128
                f[at, :] = g[:, first : first + 128].astype(BF)
        if part:
            a = g[:, full * 128 : full * 128 + 128]
            b = g[:, fp + full * 128 : fp + full * 128 + 128]
            at = rows(base_g + 2 * full * D + j * 256, 256, 16)
            f[at, :] = (a + pltpu.roll(b, part, 1)).astype(BF)
        return carry

    lax.fori_loop(0, D // 256, glu_grad, 0)
    rings[1].reduce_send(0, first=True)

    def low_block():
        dn_rs.wait()
        for i in range(tb // 128):
            at = pl.ds(i * 128, 128)
            v = r["hidden"][at, :]
            back = norm_back(v, rms_scale(v), dn_rs.result(i * 128, 128))
            d = cot_g[rows(h * tb + i * 128, 128, 128), :].astype(F32) + back
            r["dhid"][at, :] = d
            cot_g[rows(h * tb + i * 128, 128, 128), :] = d.astype(BF)
        low_ag.start(0)
        low_ag.start(1)

    def out_block():
        lo_rs.wait()
        for i in range(tb // 128):
            at = pl.ds(i * 128, 128)
            r["lo_cross"][at, :] = (r["hidden"][at, :] + lo_rs.result(i * 128, 128)).astype(BF)
        copy = pltpu.make_async_copy(r["lo_cross"], r["layer_out"], lsem.at[0])
        copy.start()
        return copy

    def low_arrive():
        for k in range(2):
            low_ag.pass_on(k)
        for k in range(2):
            low_ag.wait_beside(k)
            low_ag.wait_relay(k)

    own_out = pl.ds(pl.multiple_of(h * LOCAL, LOCAL), LOCAL)

    def mix_back(b, carry):
        at = rows(b * 256, 256, 256)
        low = cot_g[at, :]
        a = [att[k, at, :].astype(F32) for k in range(PARTS)]
        ssq = sum(jnp.sum(v * v, axis=-1, keepdims=True) for v in a)
        scale = lax.rsqrt(ssq * (1.0 / D) + EPSILON)
        inner = jnp.zeros((256, 1), F32)
        for k in range(PARTS):
            g = gate[k, at, :].astype(F32)
            e = dot_nt(low, r["wout"][pl.ds(k * LOCAL, LOCAL), :]) * (g * sigmoid(g))
            inner += jnp.sum(e * (a[k] * scale), axis=-1, keepdims=True)
        inner = inner * (1.0 / D)
        g = gate[h, at, :].astype(F32)
        sig = sigmoid(g)
        normed = att[h, at, :].astype(F32) * scale
        dm = dot_nt(low, r["wout"][own_out, :])
        slope = sig + g * sig * (1.0 - sig)
        r["dproj"][at, pl.ds(3 * LOCAL, LOCAL)] = (dm * normed * slope).astype(BF)
        r["datt"][at, :] = (scale * (dm * (g * sig) - normed * inner)).astype(BF)
        return carry

    base_r = sz.base[2]

    def out_grad():
        g = dot_tn(mixed[h], cot_g[...]).astype(BF)
        for k in range(D // 128):
            f[pl.ds(base_r + k * LOCAL, LOCAL), :] = g[:, k * 128 : (k + 1) * 128]

    def swish_slope(v):
        sig = sigmoid(v)
        return sig + v * sig * (1.0 - sig)

    def query_back(e, i):
        at = pl.ds(i * 256, 256)
        da = r["datt"][at, rows(e * HEAD_DIM, HEAD_DIM, HEAD_DIM)]
        total = jnp.zeros((256, 2 * HEAD_DIM), F32)
        for j in range(i + 1):
            near = pl.ds(j * 256, 256)
            v = r["raw"][near, rows(value_at + e * HEAD_DIM, HEAD_DIM, HEAD_DIM)]
            w = (dot_nt(da, v) * r["decay"][e, i - j]).astype(BF)
            r["weights"][at, near] = w
            total += dot(w, r["kpos"][e, near, :])
        lanes = rows(e * HEAD_DIM, HEAD_DIM, HEAD_DIM)
        co, si = r["cosine"][at, :], r["sine"][at, :]
        d = total[:, :HEAD_DIM] * co + total[:, HEAD_DIM:] * si
        raw = r["raw"][at, lanes].astype(F32)
        r["dproj"][at, lanes] = (d * swish_slope(raw)).astype(BF)

    def key_back(e, j):
        at = pl.ds(j * 256, 256)
        below = pl.ds(j * 256, t_all - j * 256)
        dk = dot_tn(r["weights"][below, at], r["qpos"][e, below, :])
        da = r["datt"][below, rows(e * HEAD_DIM, HEAD_DIM, HEAD_DIM)]
        dv = dot_tn(r["scores"][e, below, at], da)
        lanes = rows(LOCAL + e * HEAD_DIM, HEAD_DIM, HEAD_DIM)
        co, si = r["cosine"][at, :], r["sine"][at, :]
        d = dk[:, :HEAD_DIM] * co + dk[:, HEAD_DIM:] * si
        raw = r["raw"][at, lanes].astype(F32)
        r["dproj"][at, lanes] = (d * swish_slope(raw)).astype(BF)
        r["dproj"][at, rows(value_at + e * HEAD_DIM, HEAD_DIM, HEAD_DIM)] = dv.astype(BF)

    def head_back(e, carry):
        for i in range(blocks):
            query_back(e, i)
        for j in range(blocks):
            key_back(e, j)
        return carry

    base_q = base_r + (D // 128) * LOCAL

    def qkvu_grad(j, carry):
        g = dot_tn(r["n1"][:, rows(j * 256, 256, 256)], r["dproj"][...]).astype(BF)
        for k in range(D // 128):
            f[rows(base_q + k * D + j * 256, 256, 16), :] = g[:, k * 128 : (k + 1) * 128]
        return carry

    def one_part(b, carry):
        at = rows(b * 256, 256, 256)
        back = dot_nt(r["dproj"][at, pl.ds(0, 3 * LOCAL)], r["wqkv"][...])
        back += dot_nt(r["dproj"][at, pl.ds(3 * LOCAL, LOCAL)], r["wgate"][:, mine])
        r["lo_part"][at, :] = back.astype(BF)
        return carry

    own_tok = pltpu.make_async_copy(tok, r["weights"].at[pl.ds(0, tb), :], lsem.at[5])

    def last_block():
        one_rs.wait()
        own_tok.wait()
        for i in range(tb // 128):
            at = pl.ds(i * 128, 128)
            v = r["weights"][at, :].astype(F32)
            back = norm_back(v, rms_scale(v), one_rs.result(i * 128, 128))
            r["dhid"][at, :] = r["dhid"][at, :] + back
        copy = pltpu.make_async_copy(r["dhid"], r["grad_tokens"], lsem.at[1])
        copy.start()
        return copy

    def loop(lo, hi, body):
        lax.fori_loop(lo, hi, body, 0)

    def first_sums():
        loop(blocks // 2, blocks, partials)
        cot_ag.drain()
        dn_rs.start()
        lo_rs.start()

    def rest_sends():
        for ring in rings[2:]:
            ring.reduce_send(0, first=True)

    def input_sums():
        loop(0, blocks, one_part)
        one_rs.start()
        own_tok.start()

    outs = ctx.outs
    plan = {
        0: ((lambda: loop(0, blocks // 2, partials),), (first_sums,)),
        1: ((), (dn_rs.middle,)),
        3: ((), (low_block,)),
        6: ((low_arrive, lo_rs.middle), (lambda: loop(0, blocks, mix_back),)),
        7: (
            (out_grad, lambda: loop(0, 2, head_back)),
            (lambda: loop(0, D // 256, qkvu_grad), rest_sends),
        ),
        9: ((), (lambda: outs.append(out_block()), lo_rs.drain)),
        10: ((), (input_sums,)),
        11: ((), (one_rs.middle,)),
        13: ((), (lambda: outs.append(last_block()),)),
    }
    assert blocks == 4
    total = 2 * (seq - 1)
    if seq > 16:
        for slot in sorted(plan):
            for piece in plan[slot][0] + plan[slot][1]:
                piece()
        for ring in rings:
            ring.all_steps()
        copy = pltpu.make_async_copy(f, r["f_out"], lsem.at[2])
        copy.start()
        outs.append(copy)
    else:
        done = [0]

        def rest_step():
            if done[0] < total:
                for ring in rings[2:]:
                    ring.step(done[0])
                done[0] += 1

        for slot in range(max(total, max(plan) + 1)):
            for i in range(2):
                if slot > 7:
                    rest_step()
                if slot < total:
                    rings[i].step(slot)
                for piece in plan.get(slot, ((), ()))[i]:
                    piece()
        while done[0] < total:
            rest_step()

    for ag in (att_ag, low_ag):
        ag.drain()
    dn_rs.drain()
    one_rs.drain()
    for ring in rings:
        ring.drain()
    for copy in outs:
        copy.wait()


def main_call(sz, tokens, w_qkvu, w_out, w_glu, w_down, cotangent):
    any_spec = pl.BlockSpec(memory_space=pl.ANY)
    t, tb, fp, seq = sz.t, sz.tb, sz.fp, sz.seq
    scratch = dict(
        tok_g=pltpu.VMEM((t, D), BF),
        cot_g=pltpu.VMEM((t, D), BF),
        n1=pltpu.VMEM((t, D), BF),
        raw=pltpu.VMEM((t, 3 * LOCAL), BF),
        wqkv=pltpu.VMEM((D, 3 * LOCAL), BF),
        wgate=pltpu.VMEM((D, D), BF),
        wout=pltpu.VMEM((D, D), BF),
        wglu=pltpu.VMEM((D, 2 * fp), BF),
        wdown=pltpu.VMEM((fp, D), BF),
        qpos=pltpu.VMEM((2, t, 2 * HEAD_DIM), BF),
        kpos=pltpu.VMEM((2, t, 2 * HEAD_DIM), BF),
        scores=pltpu.VMEM((2, t, t), BF),
        weights=pltpu.VMEM((t, t), BF),
        decay=pltpu.VMEM((2, t // 256, 256, 256), F32),
        cosine=pltpu.VMEM((t, HEAD_DIM), F32),
        sine=pltpu.VMEM((t, HEAD_DIM), F32),
        att=pltpu.VMEM((PARTS, t, LOCAL), BF),
        gate=pltpu.VMEM((PARTS, t, LOCAL), BF),
        mixed=pltpu.VMEM((PARTS, t, LOCAL), BF),
        hidden=pltpu.VMEM((tb, D), F32),
        product=pltpu.VMEM((t, fp), BF),
        dpair=pltpu.VMEM((t, 2 * fp), BF),
        dn_part=pltpu.VMEM((t, D), BF),
        dn_near=pltpu.VMEM((2, tb, D), BF),
        dn_cross=pltpu.VMEM((tb, D), BF),
        lo_near=pltpu.VMEM((2, tb, D), BF),
        lo_cross=pltpu.VMEM((tb, D), BF),
        dhid=pltpu.VMEM((tb, D), F32),
        f=pltpu.VMEM((sz.total, 128), BF),
        slots0=pltpu.VMEM((2, seq - 1, sz.chunk[0], 128), BF),
        slots1=pltpu.VMEM((2, seq - 1, sz.chunk[1], 128), BF),
        slots2=pltpu.VMEM((2, seq - 1, sz.chunk[2], 128), BF),
        slots3=pltpu.VMEM((2, seq - 1, sz.chunk[3], 128), BF),
        gsend=pltpu.SemaphoreType.DMA((48,)),
        grecv=pltpu.SemaphoreType.DMA((48,)),
        rsend=pltpu.SemaphoreType.DMA((4, 2, 2 * (seq - 1))),
        rrecv=pltpu.SemaphoreType.DMA((4, 2, 2 * (seq - 1))),
        psem=pltpu.SemaphoreType.DMA((4, 2, min(seq, 16))),
        lsem=pltpu.SemaphoreType.DMA((24,)),
    )
    if seq > 16:
        for i in range(4):
            del scratch["slots%d" % i]
        scratch["slots"] = pltpu.VMEM((2, seq - 1, max(sz.chunk), 128), BF)
    assert 2 * fp >= D + LOCAL and tb == 256
    names = ["tok", "w_qkvu", "w_out", "w_glu", "w_down", "cot", "layer_out", "grad_tokens", "f_out"]
    names += list(scratch)

    def kernel(*refs):
        named = dict(zip(names, refs))
        named["n2"] = named["weights"]
        for i in range(4 if seq > 16 else 0):
            named["slots%d" % i] = named["slots"].at[:, :, pl.ds(0, sz.chunk[i]), :]
        named["lo_part"] = named["tok_g"]
        named["one_near"], named["one_cross"] = named["dn_near"], named["dn_cross"]
        named["dproj"] = named["dpair"].at[:, pl.ds(0, D)]
        named["datt"] = named["dpair"].at[:, pl.ds(D, LOCAL)]
        layer_kernel(sz, list(named), *named.values())

    return pl.pallas_call(
        kernel,
        name="layer",
        out_shape=(
            jax.ShapeDtypeStruct((tb, D), BF),
            jax.ShapeDtypeStruct((tb, D), F32),
            jax.ShapeDtypeStruct((sz.total, 128), BF),
        ),
        in_specs=[any_spec] * 6,
        out_specs=(any_spec,) * 3,
        scratch_shapes=list(scratch.values()),
        compiler_params=pltpu.CompilerParams(
            collective_id=0, has_side_effects=True, vmem_limit_bytes=67043328
        ),
    )(tokens, w_qkvu, w_out, w_glu, w_down, cotangent)


def unpack_kernel(sz, flat, lo_in, gt_in, lo_out, gt_out, qkvu, out, glu, down, *scratch):
    buf, lo_b, gt_b, qkvu_b, out_b, glu_b, down_b, sem = scratch
    fs, full = sz.fs, sz.full_tiles
    part = fs % 128
    count = [0]

    def start(src, dst):
        copy = pltpu.make_async_copy(src, dst, sem.at[count[0]])
        copy.start()
        count[0] += 1
        return copy

    def fetch(first, size):
        return start(flat.at[pl.ds(first, size), :], buf.at[pl.ds(first, size), :])

    def tile(first, size):
        return buf[pl.ds(first, size), :].astype(F32)

    base_g, base_o = sz.base[1], sz.base[2]
    base_q = base_o + (D // 128) * LOCAL
    half = full * D
    down_in = [fetch(k * 4 * fs, 4 * fs) for k in range(2)]
    glu_in = [fetch(base_g, half), fetch(base_g + 2 * half, D) if part else None]
    glu_in.append(fetch(base_g + half, half))
    out_in = fetch(base_o, (D // 128) * LOCAL)
    qkvu_in = [fetch(base_q + k * 2 * D, 2 * D) for k in range(4)]
    lo_copy, gt_copy = start(lo_in, lo_b), start(gt_in, gt_b)
    outs = []
    for k in range(2):
        down_in[k].wait()
        for i in range(4 * k, 4 * k + 4):
            down_b[:, pl.ds(i * 128, 128)] = tile(i * fs, fs)
        lanes = pl.ds(k * 512, 512)
        outs.append(start(down_b.at[:, lanes], down.at[:, lanes]))
    if part:
        glu_in[1].wait()
    for k in range(2):
        glu_in[2 * k].wait()
        for i in range(full):
            glu_b[k, :, pl.ds(i * 128, 128)] = tile(base_g + (k * full + i) * D, D)
        if part:
            both = tile(base_g + 2 * half, D)
            both = pltpu.roll(both, 128 - part, 1) if k else both
            glu_b[k, :, pl.ds(full * 128, part)] = both[:, :part]
        outs.append(start(glu_b.at[k], glu.at[k]))
    out_in.wait()
    for i in range(D // 128):
        out_b[:, pl.ds(i * 128, 128)] = tile(base_o + i * LOCAL, LOCAL)
    outs.append(start(out_b, out))
    for k in range(4):
        qkvu_in[k].wait()
        for i in range(2):
            qkvu_b[k, :, pl.ds(i * 128, 128)] = tile(base_q + (2 * k + i) * D, D)
        outs.append(start(qkvu_b.at[k], qkvu.at[k]))
    lo_copy.wait()
    outs.append(start(lo_b, lo_out))
    gt_copy.wait()
    outs.append(start(gt_b, gt_out))
    for copy in outs:
        copy.wait()


def unpack(sz, flat, layer_out, grad_tokens):
    any_spec = pl.BlockSpec(memory_space=pl.ANY)
    outs = (
        jax.ShapeDtypeStruct((sz.tb, D), BF),
        jax.ShapeDtypeStruct((sz.tb, D), F32),
        jax.ShapeDtypeStruct((4, D, LOCAL), F32),
        jax.ShapeDtypeStruct((LOCAL, D), F32),
        jax.ShapeDtypeStruct((2, D, sz.fs), F32),
        jax.ShapeDtypeStruct((sz.fs, D), F32),
    )
    return pl.pallas_call(
        functools.partial(unpack_kernel, sz),
        name="unpack",
        out_shape=outs,
        in_specs=[any_spec] * 3,
        out_specs=(any_spec,) * 6,
        scratch_shapes=[pltpu.VMEM((sz.total, 128), BF)]
        + [pltpu.VMEM(v.shape, v.dtype) for v in outs]
        + [pltpu.SemaphoreType.DMA((32,))],
        compiler_params=pltpu.CompilerParams(vmem_limit_bytes=48 << 20),
    )(flat, layer_out, grad_tokens)


def per_device(tokens, seq_lengths, w_qkvu, w_out, w_glu, w_down, cotangent):
    assert seq_lengths.shape == (1, 1) and lax.axis_size("head") == PARTS
    sz = Sizes(lax.axis_size("seq"), tokens.shape[0], w_down.shape[0])
    layer_out, grad_tokens, flat = main_call(sz, tokens, w_qkvu, w_out, w_glu, w_down, cotangent)
    return tuple(unpack(sz, flat, layer_out, grad_tokens))


def solution(mesh):
    return jax.shard_map(
        per_device,
        mesh=mesh,
        in_specs=(
            P(("seq", "head"), None),
            P("seq", None),
            P(),
            P(),
            P(),
            P(),
            P(("seq", "head"), None),
        ),
        out_specs=(
            P(("seq", "head"), None),
            P(("seq", "head"), None),
            P(None, None, "head"),
            P("head", None),
            P(None, None, "head"),
            P("head", None),
        ),
        check_vma=False,
    )
```

profile of v0, /device:TPU:0, one launch (start us, length us, event | category | flops | bytes accessed | tf_op | source)
XLA Modules:
  0.0 213.2 jit_solution(15056498978904907608)
XLA Ops:
  0.6 196.5 %layer.1 = (bf16[256,1024]{1,0:T(8,128)(2,1)}, f32[256,1024]{1,0:T(8,128)}, bf16[27136,128]{1,0:T(8,128)(2,1)}) custom-call(bf16[256,1024]{1,0:T(8,128)(2,1)} %refs_0_.1, bf16[4,1024,1024]{2,1,0:T(8,128)(2,1)} %refs_1_.1, bf16[1024,1024]{1,0:T(8,128)(2,1)} %refs_2_.1, bf16[2,1024,2816]{2,1,0:T(8,128)(2,1)} %refs_3_.1, bf16[2816,1024]{1,0:T(8,128)(2,1)} %refs_4_.1, ...), custom_call_target="tpu_custom_call" | custom-call | tf_op jit(solution)/shard_map/layer/pallas_call | solution.py:869
  197.1 0.0 copy-start
  197.1 1.2 copy-done
  198.3 0.0 copy-start.1
  198.3 1.0 copy-done.1
  199.4 7.5 %unpack.1 = (bf16[256,1024]{1,0:T(8,128)(2,1)}, f32[256,1024]{1,0:T(8,128)}, f32[4,1024,256]{2,1,0:T(8,128)}, f32[256,1024]{1,0:T(8,128)}, f32[2,1024,704]{2,1,0:T(8,128)}, /*index=5*/f32[704,1024]{1,0:T(8,128)}) custom-call(bf16[27136,128]{1,0:T(8,128)(2,1)} %get-tuple-element.9.flat, bf16[256,1024]{1,0:T(8,128)(2,1)S(1)} %copy-done.1, f32[256,1024]{1,0:T(8,128)S(1)} %copy-done), custom_call_target="tpu_custom_call" | custom-call | tf_op jit(solution)/shard_map/unpack/pallas_call | solution.py:958
  206.9 6.4 %copy.12 = f32[2,1024,704]{1,2,0:T(8,128)} copy(f32[2,1024,704]{2,1,0:T(8,128)} %get-tuple-element.16) | data formatting | bytes 11534336 | tf_op jit(solution)/shard_map/unpack/pallas_call | solution.py:958
Async XLA Ops:
  197.1 1.2 copy-start
  198.3 1.0 copy-start.1
where the time goes:
time: 213 us
  Pallas kernels  204 us (96%)
  local copies, waits for them, and re-layouts  8.62 us (4%)
    pallas_call x1, Pallas kernels, main_call(): pl.pallas_call(kernel, name='layer', out_shape=(jax.ShapeDtypeStruct((tb,...  196 us
    pallas_call x1, Pallas kernels, unpack(): pl.pallas_call(functools.partial(unpack_kernel, sz), name='unpack', out_s...  7.49 us
    pallas_call x1, local copies, waits for them, and re-layouts, unpack(): pl.pallas_call(functools.partial(unpack_kernel, sz), name='unpack', out_s...  6.36 us

commit v1 on v0

--- a/solution.py
+++ b/solution.py
@@ -58,11 +58,9 @@
         self.t = block * PARTS
         self.fs = ff // PARTS
         self.fp = round_up(self.fs, 256)
-        self.full_tiles = self.fs // 128
-        self.glu_tiles = 2 * self.full_tiles + (1 if self.fs % 128 else 0)
         rest = (D // 128) * LOCAL + 4 * (LOCAL // 128) * D
         chunk = lambda n: round_up(-(-n // (2 * seq)), 16)
-        self.chunk = [chunk((D // 128) * self.fs), chunk(self.glu_tiles * D), chunk(rest // 2)]
+        self.chunk = [chunk((D // 128) * self.fs), chunk(2 * (D // 128) * self.fs), chunk(rest // 2)]
         self.chunk.append(chunk(rest - 2 * seq * self.chunk[2]))
         self.base = [2 * seq * sum(self.chunk[:i]) for i in range(5)]
         self.total = self.base[4]
@@ -583,23 +581,19 @@
     rings[0].reduce_send(0, first=True)
 
     base_g = sz.base[1]
-    full = sz.full_tiles
-
-    def glu_grad(j, carry):
-        g = dot_tn(r["n2"][:, rows(j * 256, 256, 256)], r["dpair"][...])
-        for k in range(2):
-            for i in range(full):
-                at = rows(base_g + (k * full + i) * D + j * 256, 256, 16)
-                first = k * fp + i * 128
-                f[at, :] = g[:, first : first + 128].astype(BF)
-        if part:
-            a = g[:, full * 128 : full * 128 + 128]
-            b = g[:, fp + full * 128 : fp + full * 128 + 128]
-            at = rows(base_g + 2 * full * D + j * 256, 256, 16)
-            f[at, :] = (a + pltpu.roll(b, part, 1)).astype(BF)
+
+    def glu_grad(k, carry):
+        first = base_g + k * (D // 128) * fs
+        for j in range(fp // 256):
+            size = min(256, fs - j * 256)
+            lanes = rows(k * fp + j * 256, 256, 256)
+            g = dot_tn(r["dpair"][:, lanes], r["n2"][...]).astype(BF)
+            for i in range(D // 128):
+                at = rows(first + i * fs + j * 256, size, 16)
+                f[at, :] = g[:size, i * 128 : (i + 1) * 128]
         return carry
 
-    lax.fori_loop(0, D // 256, glu_grad, 0)
+    lax.fori_loop(0, 2, glu_grad, 0)
     rings[1].reduce_send(0, first=True)
 
     def low_block():
@@ -885,8 +879,7 @@
 
 def unpack_kernel(sz, flat, lo_in, gt_in, lo_out, gt_out, qkvu, out, glu, down, *scratch):
     buf, lo_b, gt_b, qkvu_b, out_b, glu_b, down_b, sem = scratch
-    fs, full = sz.fs, sz.full_tiles
-    part = fs % 128
+    fs = sz.fs
     count = [0]
 
     def start(src, dst):
@@ -903,10 +896,9 @@
 
     base_g, base_o = sz.base[1], sz.base[2]
     base_q = base_o + (D // 128) * LOCAL
-    half = full * D
+    half = (D // 128) * fs
     down_in = [fetch(k * 4 * fs, 4 * fs) for k in range(2)]
-    glu_in = [fetch(base_g, half), fetch(base_g + 2 * half, D) if part else None]
-    glu_in.append(fetch(base_g + half, half))
+    glu_in = [fetch(base_g + k * half, half) for k in range(2)]
     out_in = fetch(base_o, (D // 128) * LOCAL)
     qkvu_in = [fetch(base_q + k * 2 * D, 2 * D) for k in range(4)]
     lo_copy, gt_copy = start(lo_in, lo_b), start(gt_in, gt_b)
@@ -917,16 +909,10 @@
             down_b[:, pl.ds(i * 128, 128)] = tile(i * fs, fs)
         lanes = pl.ds(k * 512, 512)
         outs.append(start(down_b.at[:, lanes], down.at[:, lanes]))
-    if part:
-        glu_in[1].wait()
     for k in range(2):
-        glu_in[2 * k].wait()
-        for i in range(full):
-            glu_b[k, :, pl.ds(i * 128, 128)] = tile(base_g + (k * full + i) * D, D)
-        if part:
-            both = tile(base_g + 2 * half, D)
-            both = pltpu.roll(both, 128 - part, 1) if k else both
-            glu_b[k, :, pl.ds(full * 128, part)] = both[:, :part]
+        glu_in[k].wait()
+        for i in range(D // 128):
+            glu_b[k, :, pl.ds(i * 128, 128)] = tile(base_g + k * half + i * fs, fs)
         outs.append(start(glu_b.at[k], glu.at[k]))
     out_in.wait()
     for i in range(D // 128):
@@ -952,7 +938,7 @@
         jax.ShapeDtypeStruct((sz.tb, D), F32),
         jax.ShapeDtypeStruct((4, D, LOCAL), F32),
         jax.ShapeDtypeStruct((LOCAL, D), F32),
-        jax.ShapeDtypeStruct((2, D, sz.fs), F32),
+        jax.ShapeDtypeStruct((2, sz.fs, D), F32),
         jax.ShapeDtypeStruct((sz.fs, D), F32),
     )
     return pl.pallas_call(
@@ -964,7 +950,7 @@
         scratch_shapes=[pltpu.VMEM((sz.total, 128), BF)]
         + [pltpu.VMEM(v.shape, v.dtype) for v in outs]
         + [pltpu.SemaphoreType.DMA((32,))],
-        compiler_params=pltpu.CompilerParams(vmem_limit_bytes=48 << 20),
+        compiler_params=pltpu.CompilerParams(vmem_limit_bytes=67043328),
     )(flat, layer_out, grad_tokens)
 
 
@@ -972,7 +958,9 @@
     assert seq_lengths.shape == (1, 1) and lax.axis_size("head") == PARTS
     sz = Sizes(lax.axis_size("seq"), tokens.shape[0], w_down.shape[0])
     layer_out, grad_tokens, flat = main_call(sz, tokens, w_qkvu, w_out, w_glu, w_down, cotangent)
-    return tuple(unpack(sz, flat, layer_out, grad_tokens))
+    outs = list(unpack(sz, flat, layer_out, grad_tokens))
+    outs[4] = outs[4].transpose(0, 2, 1)
+    return tuple(outs)
 
 
 def solution(mesh):

time: 213 us -> 205 us (0.962)
  local copies, waits for them, and re-layouts: 8.62 us -> 0 us
    pallas_call x1 -> x0, local copies, waits for them, and re-layouts: 6.36 us -> none  [unpack(): pl.pallas_call(functools.partial(unpack_kernel, sz), name='unpack', out_s...]
    unnamed x4 -> x0, local copies, waits for them, and re-layouts: 2.26 us -> none
where the time goes in v1:
time: 205 us; the launch traced here: 204 us
  Pallas kernels  204 us (100%)
    pallas_call x1, Pallas kernels, main_call(): pl.pallas_call(kernel, name='layer', out_shape=(jax.ShapeDtypeStruct((tb,...  196 us
    pallas_call x1, Pallas kernels, unpack(): pl.pallas_call(functools.partial(unpack_kernel, sz), name='unpack', out_s...  7.88 us

profile of v1, /device:TPU:0, one launch (start us, length us, event | category | flops | bytes accessed | tf_op | source)
XLA Modules:
  0.0 204.4 jit_solution(4237783526191000395)
XLA Ops:
  0.6 195.7 %layer.1 = (bf16[256,1024]{1,0:T(8,128)(2,1)}, f32[256,1024]{1,0:T(8,128)}, bf16[27136,128]{1,0:T(8,128)(2,1)}) custom-call(bf16[256,1024]{1,0:T(8,128)(2,1)} %refs_0_.1, bf16[4,1024,1024]{2,1,0:T(8,128)(2,1)} %refs_1_.1, bf16[1024,1024]{1,0:T(8,128)(2,1)} %refs_2_.1, bf16[2,1024,2816]{2,1,0:T(8,128)(2,1)} %refs_3_.1, bf16[2816,1024]{1,0:T(8,128)(2,1)} %refs_4_.1, ...), custom_call_target="tpu_custom_call" | custom-call | tf_op jit(solution)/shard_map/layer/pallas_call | solution.py:863
  196.4 7.9 %unpack.1 = (bf16[256,1024]{1,0:T(8,128)(2,1)}, f32[256,1024]{1,0:T(8,128)}, f32[4,1024,256]{2,1,0:T(8,128)}, f32[256,1024]{1,0:T(8,128)}, f32[2,704,1024]{2,1,0:T(8,128)}, /*index=5*/f32[704,1024]{1,0:T(8,128)}) custom-call(bf16[27136,128]{1,0:T(8,128)(2,1)} %get-tuple-element.15.flat, bf16[256,1024]{1,0:T(8,128)(2,1)} %get-tuple-element.16.lo_in, ...), custom_call_target="tpu_custom_call" | custom-call | tf_op jit(solution)/shard_map/unpack/pallas_call | solution.py:944

commit v2 on v1

--- a/solution.py
+++ b/solution.py
@@ -60,10 +60,10 @@
         self.fp = round_up(self.fs, 256)
         rest = (D // 128) * LOCAL + 4 * (LOCAL // 128) * D
         chunk = lambda n: round_up(-(-n // (2 * seq)), 16)
-        self.chunk = [chunk((D // 128) * self.fs), chunk(2 * (D // 128) * self.fs), chunk(rest // 2)]
-        self.chunk.append(chunk(rest - 2 * seq * self.chunk[2]))
-        self.base = [2 * seq * sum(self.chunk[:i]) for i in range(5)]
-        self.total = self.base[4]
+        self.chunk = [chunk((D // 128) * self.fs)] * 3 + [chunk(rest // 2)]
+        self.chunk.append(chunk(rest - 2 * seq * self.chunk[3]))
+        self.base = [2 * seq * sum(self.chunk[:i]) for i in range(6)]
+        self.total = self.base[5]
 
 
 class Gather:
@@ -184,8 +184,8 @@
         return pltpu.make_async_remote_copy(
             src_ref=src,
             dst_ref=dst,
-            send_sem=c.rsend.at[self.index, d, step],
-            recv_sem=c.rrecv.at[self.index, d, step],
+            send_sem=c.rsend.at[self.index, d, lax.rem(step, 2)],
+            recv_sem=c.rrecv.at[self.index, d, lax.rem(step, 2)],
             device_id=(c.right if d == 0 else c.left, c.h),
             device_id_type=MESH,
         )
@@ -193,14 +193,12 @@
     def toward(self, d, t):
         return self.ctx.p + (self.n - t if d == 0 else t)
 
-    def publish(self, d, k, j):
+    def publish(self, d, k):
         if self.n > 16:
             return
         at = self.mine(d, k)
         c = self.ctx
-        copy = pltpu.make_async_copy(c.f.at[at, :], c.f_out.at[at, :], c.psem.at[self.index, d, j])
-        copy.start()
-        c.outs.append(copy)
+        pltpu.make_async_copy(c.f.at[at, :], c.f_out.at[at, :], c.psem.at[0]).start()
 
     def reduce_copy(self, d, t, first=False):
         f = self.ctx.f
@@ -228,7 +226,7 @@
                 else:
                     self.slots[d, t, inside, :] = total.astype(BF)
             if last:
-                self.publish(d, k, self.n - 1)
+                self.publish(d, k)
 
     def spread_copy(self, d, t):
         spot = self.ctx.f.at[self.mine(d, self.toward(d, t) + (1 if d == 0 else self.n - 1)), :]
@@ -242,66 +240,52 @@
         for d in range(2):
             self.spread_copy(d, t).wait_recv()
             if isinstance(t, int):
-                self.publish(d, self.toward(d, t), t)
-
-    def leave(self):
+                self.publish(d, self.toward(d, t))
+
+    def left(self, step):
         for d in range(2):
-            self.reduce_copy(d, 0, first=True).wait_send()
+            if isinstance(step, int) and step >= self.n - 1:
+                self.spread_copy(d, step - self.n + 1).wait_send()
+            else:
+                self.reduce_copy(d, step, first=True).wait_send()
 
     def step(self, t):
         last = self.n - 2
         if t <= last:
             self.reduce_take(t, last=t == last)
-            if t == 0:
-                self.leave()
-            if t < last:
-                self.reduce_send(t + 1)
-            else:
-                self.spread_send(0)
         else:
-            t -= self.n - 1
-            self.spread_take(t)
-            if t < last:
-                self.spread_send(t + 1)
+            self.spread_take(t - self.n + 1)
+        if t > 0:
+            self.left(t - 1)
+        if t < last:
+            self.reduce_send(t + 1)
+        elif t < 2 * last + 1:
+            self.spread_send(t - last)
 
     def all_steps(self):
         last = self.n - 2
+        self.step(0)
 
         def turn(t, carry):
             self.reduce_take(t)
+            self.left(t - 1)
             self.reduce_send(t + 1)
             return carry
 
-        self.leave()
-        lax.fori_loop(0, last, turn, 0)
-        self.reduce_take(last, last=True)
-        self.spread_send(0)
+        lax.fori_loop(1, last, turn, 0)
+        self.step(last)
 
         def pass_on(t, carry):
             self.spread_take(t)
+            self.left(last + t)
             self.spread_send(t + 1)
             return carry
 
         lax.fori_loop(0, last, pass_on, 0)
-        self.spread_take(last)
+        self.step(2 * last + 1)
 
     def drain(self):
-        if self.n > 16:
-
-            def one(t, carry):
-                for d in range(2):
-                    self.reduce_copy(d, t + 1, first=True).wait_send()
-                    self.spread_copy(d, t).wait_send()
-                return carry
-
-            lax.fori_loop(0, self.n - 2, one, 0)
-        else:
-            for t in range(1, self.n - 1):
-                for d in range(2):
-                    self.reduce_copy(d, t, first=True).wait_send()
-                    self.spread_copy(d, t - 1).wait_send()
-        for d in range(2):
-            self.spread_copy(d, self.n - 2).wait_send()
+        self.left(2 * self.n - 3)
 
 
 class Ctx:
@@ -345,6 +329,10 @@
         loads.append(copy)
         return copy
 
+    barrier = pltpu.get_barrier_semaphore()
+    for peer in ((s, ctx.sib), (s, ctx.yp), (ctx.right, h), (ctx.left, h)):
+        pl.semaphore_signal(barrier, inc=1, device_id=peer, device_id_type=MESH)
+
     mine = pl.ds(pl.multiple_of(h * LOCAL, LOCAL), LOCAL)
     own_rows = rows(h * tb, tb, tb)
     tok_in = load(tok, tok_g.at[own_rows, :])
@@ -354,20 +342,15 @@
     gate_in = load(r["w_qkvu"].at[3], r["wgate"])
     out_in = load(r["w_out"], r["wout"])
     down_in = load(r["w_down"].at[rows(h * fs, fs, 64), :], r["wdown"].at[pl.ds(0, fs), :])
-    glu_in = []
     window = y * (2 * fs) + c * (fs - fs % 128)
     tiles = fp // 128
     for k in range(2):
         for j in range(tiles):
             lane = pl.ds(pl.multiple_of(window + j * 128, 128), 128)
-            glu_in.append(
-                load(r["w_glu"].at[k, :, lane], f.at[pl.ds((k * tiles + j) * D, D), :])
-            )
+            staged = f.at[pl.ds((k * tiles + j) * D, D), :]
+            pltpu.make_async_copy(r["w_glu"].at[k, :, lane], staged, lsem.at[8]).start()
     cot_in = load(cot, cot_g.at[own_rows, :])
 
-    barrier = pltpu.get_barrier_semaphore()
-    for peer in ((s, ctx.sib), (s, ctx.yp), (ctx.right, h), (ctx.left, h)):
-        pl.semaphore_signal(barrier, inc=1, device_id=peer, device_id_type=MESH)
     pl.semaphore_wait(barrier, 4)
 
     hb = tb // 2
@@ -387,12 +370,13 @@
     )
     blocks = t_all // 256
     att_place = lambda b, k: att.at[b, pl.ds(k * 256, 256), :]
-    att_ag = Gather(ctx, blocks, lambda k: att_place(h, k), att_place, 33)
+    att_ag = Gather(ctx, blocks, lambda k: att_place(h, k), att_place, 18)
     low_place = lambda b, k: cot_g.at[rows(b * tb + k * hb, hb, hb), :]
-    low_ag = Gather(ctx, 2, lambda k: low_place(h, k), low_place, 18)
-
-    for k in range(2):
-        token_ag.start(k)
+    low_ag = Gather(ctx, 2, lambda k: low_place(h, k), low_place, 0)
+
+    for ag in (token_ag, cot_ag):
+        for k in range(2):
+            ag.start(k)
 
     lane = lax.broadcasted_iota(jnp.int32, (32, HEAD_DIM), 1).astype(F32)
     step = lax.broadcasted_iota(jnp.int32, (32, HEAD_DIM), 0).astype(F32)
@@ -419,8 +403,8 @@
             r["decay"][e, k] = jnp.where(distance >= 0, value, 0.0)
 
     r["wdown"][pl.ds(fs, fp - fs), :] = jnp.zeros((fp - fs, D), BF)
-    for one in glu_in:
-        one.wait()
+    staged = f.at[pl.ds(0, 2 * tiles * D), :]
+    pltpu.make_async_copy(staged, staged, lsem.at[8]).wait()
     part = fs % 128
     low_lanes = lax.broadcasted_iota(jnp.int32, (256, 128), 1) < 128 - part
     keep = lax.broadcasted_iota(jnp.int32, (256, 128), 1) < part if part else None
@@ -474,8 +458,6 @@
         def _():
             for i in range(2):
                 token_ag.pass_on(i)
-            for i in range(2):
-                cot_ag.start(i)
 
         @pl.when(k == 3)
         def _():
@@ -526,7 +508,8 @@
 
             @pl.when(b == k)
             def _():
-                att_ag.pass_on(k)
+                if k + 1 < blocks:
+                    att_ag.pass_on(k + 1)
                 att_ag.wait_beside(k)
                 att_ag.wait_relay(k)
 
@@ -565,12 +548,13 @@
         return carry
 
     token_ag.drain()
+    att_ag.pass_on(0)
     lax.fori_loop(0, blocks, mlp, 0)
 
-    dn_rs = Scatter(ctx, r["dn_part"], r["dn_near"], r["dn_cross"], 24)
-    lo_rs = Scatter(ctx, r["lo_part"], r["lo_near"], r["lo_cross"], 27)
-    one_rs = Scatter(ctx, r["lo_part"], r["one_near"], r["one_cross"], 30)
-    rings = [Ring(ctx, i, r["slots%d" % i]) for i in range(4)]
+    dn_rs = Scatter(ctx, r["dn_part"], r["dn_near"], r["dn_cross"], 12)
+    lo_rs = Scatter(ctx, r["lo_part"], r["lo_near"], r["lo_cross"], 15)
+    one_rs = Scatter(ctx, r["lo_part"], r["one_near"], r["one_cross"], 12)
+    rings = [Ring(ctx, i, r["slots%d" % i]) for i in range(5)]
 
     base = sz.base[0]
     for j in range(fp // 256):
@@ -580,10 +564,8 @@
             f[pl.ds(base + k * fs + j * 256, size), :] = g[:size, k * 128 : (k + 1) * 128]
     rings[0].reduce_send(0, first=True)
 
-    base_g = sz.base[1]
-
-    def glu_grad(k, carry):
-        first = base_g + k * (D // 128) * fs
+    def glu_grad(k):
+        first = sz.base[1 + k]
         for j in range(fp // 256):
             size = min(256, fs - j * 256)
             lanes = rows(k * fp + j * 256, 256, 256)
@@ -591,10 +573,10 @@
             for i in range(D // 128):
                 at = rows(first + i * fs + j * 256, size, 16)
                 f[at, :] = g[:size, i * 128 : (i + 1) * 128]
-        return carry
-
-    lax.fori_loop(0, 2, glu_grad, 0)
-    rings[1].reduce_send(0, first=True)
+        rings[1 + k].reduce_send(0, first=True)
+
+    for k in range(2):
+        glu_grad(k)
 
     def low_block():
         dn_rs.wait()
@@ -647,7 +629,7 @@
         r["datt"][at, :] = (scale * (dm * (g * sig) - normed * inner)).astype(BF)
         return carry
 
-    base_r = sz.base[2]
+    base_r = sz.base[3]
 
     def out_grad():
         g = dot_tn(mixed[h], cot_g[...]).astype(BF)
@@ -733,11 +715,12 @@
         lo_rs.start()
 
     def rest_sends():
-        for ring in rings[2:]:
+        for ring in rings[3:]:
             ring.reduce_send(0, first=True)
 
     def input_sums():
         loop(0, blocks, one_part)
+        dn_rs.drain()
         one_rs.start()
         own_tok.start()
 
@@ -764,15 +747,13 @@
                 piece()
         for ring in rings:
             ring.all_steps()
-        copy = pltpu.make_async_copy(f, r["f_out"], lsem.at[2])
-        copy.start()
-        outs.append(copy)
+        pltpu.make_async_copy(f, r["f_out"], ctx.psem.at[0]).start()
     else:
         done = [0]
 
         def rest_step():
             if done[0] < total:
-                for ring in rings[2:]:
+                for ring in rings[3:]:
                     ring.step(done[0])
                 done[0] += 1
 
@@ -781,7 +762,8 @@
                 if slot > 7:
                     rest_step()
                 if slot < total:
-                    rings[i].step(slot)
+                    for ring in rings[:1] if i == 0 else rings[1:3]:
+                        ring.step(slot)
                 for piece in plan.get(slot, ((), ()))[i]:
                     piece()
         while done[0] < total:
@@ -789,12 +771,12 @@
 
     for ag in (att_ag, low_ag):
         ag.drain()
-    dn_rs.drain()
     one_rs.drain()
     for ring in rings:
         ring.drain()
     for copy in outs:
         copy.wait()
+    pltpu.make_async_copy(f, r["f_out"], ctx.psem.at[0]).wait()
 
 
 def main_call(sz, tokens, w_qkvu, w_out, w_glu, w_down, cotangent):
@@ -834,15 +816,16 @@
         slots1=pltpu.VMEM((2, seq - 1, sz.chunk[1], 128), BF),
         slots2=pltpu.VMEM((2, seq - 1, sz.chunk[2], 128), BF),
         slots3=pltpu.VMEM((2, seq - 1, sz.chunk[3], 128), BF),
-        gsend=pltpu.SemaphoreType.DMA((48,)),
-        grecv=pltpu.SemaphoreType.DMA((48,)),
-        rsend=pltpu.SemaphoreType.DMA((4, 2, 2 * (seq - 1))),
-        rrecv=pltpu.SemaphoreType.DMA((4, 2, 2 * (seq - 1))),
-        psem=pltpu.SemaphoreType.DMA((4, 2, min(seq, 16))),
-        lsem=pltpu.SemaphoreType.DMA((24,)),
+        slots4=pltpu.VMEM((2, seq - 1, sz.chunk[4], 128), BF),
+        gsend=pltpu.SemaphoreType.DMA((30,)),
+        grecv=pltpu.SemaphoreType.DMA((30,)),
+        rsend=pltpu.SemaphoreType.DMA((5, 2, 2)),
+        rrecv=pltpu.SemaphoreType.DMA((5, 2, 2)),
+        psem=pltpu.SemaphoreType.DMA((1,)),
+        lsem=pltpu.SemaphoreType.DMA((9,)),
     )
     if seq > 16:
-        for i in range(4):
+        for i in range(5):
             del scratch["slots%d" % i]
         scratch["slots"] = pltpu.VMEM((2, seq - 1, max(sz.chunk), 128), BF)
     assert 2 * fp >= D + LOCAL and tb == 256
@@ -852,7 +835,7 @@
     def kernel(*refs):
         named = dict(zip(names, refs))
         named["n2"] = named["weights"]
-        for i in range(4 if seq > 16 else 0):
+        for i in range(5 if seq > 16 else 0):
             named["slots%d" % i] = named["slots"].at[:, :, pl.ds(0, sz.chunk[i]), :]
         named["lo_part"] = named["tok_g"]
         named["one_near"], named["one_cross"] = named["dn_near"], named["dn_cross"]
@@ -894,11 +877,11 @@
     def tile(first, size):
         return buf[pl.ds(first, size), :].astype(F32)
 
-    base_g, base_o = sz.base[1], sz.base[2]
+    base_o = sz.base[3]
     base_q = base_o + (D // 128) * LOCAL
     half = (D // 128) * fs
     down_in = [fetch(k * 4 * fs, 4 * fs) for k in range(2)]
-    glu_in = [fetch(base_g + k * half, half) for k in range(2)]
+    glu_in = [fetch(sz.base[1 + k], half) for k in range(2)]
     out_in = fetch(base_o, (D // 128) * LOCAL)
     qkvu_in = [fetch(base_q + k * 2 * D, 2 * D) for k in range(4)]
     lo_copy, gt_copy = start(lo_in, lo_b), start(gt_in, gt_b)
@@ -912,7 +895,7 @@
     for k in range(2):
         glu_in[k].wait()
         for i in range(D // 128):
-            glu_b[k, :, pl.ds(i * 128, 128)] = tile(base_g + k * half + i * fs, fs)
+            glu_b[k, :, pl.ds(i * 128, 128)] = tile(sz.base[1 + k] + i * fs, fs)
         outs.append(start(glu_b.at[k], glu.at[k]))
     out_in.wait()
     for i in range(D // 128):

time: 205 us -> 197 us (0.961)
  Pallas kernels: 204 us -> 196 us
    pallas_call x1, Pallas kernels: 196 us -> 188 us  [main_call(): pl.pallas_call(kernel, name='layer', out_shape=(jax.ShapeDtypeStruct((tb,...]
where the time goes in v2:
time: 197 us
  Pallas kernels  196 us (99%)
    pallas_call x1, Pallas kernels, main_call(): pl.pallas_call(kernel, name='layer', out_shape=(jax.ShapeDtypeStruct((tb,...  188 us
    pallas_call x1, Pallas kernels, unpack(): pl.pallas_call(functools.partial(unpack_kernel, sz), name='unpack', out_s...  7.88 us

profile of v2, /device:TPU:0, one launch (start us, length us, event | category | flops | bytes accessed | tf_op | source)
XLA Modules:
  0.0 196.7 jit_solution(3500704517501677181)
XLA Ops:
  0.6 188.0 %layer.1 = (bf16[256,1024]{1,0:T(8,128)(2,1)}, f32[256,1024]{1,0:T(8,128)}, bf16[27136,128]{1,0:T(8,128)(2,1)}) custom-call(bf16[256,1024]{1,0:T(8,128)(2,1)} %refs_0_.1, bf16[4,1024,1024]{2,1,0:T(8,128)(2,1)} %refs_1_.1, bf16[1024,1024]{1,0:T(8,128)(2,1)} %refs_2_.1, bf16[2,1024,2816]{2,1,0:T(8,128)(2,1)} %refs_3_.1, bf16[2816,1024]{1,0:T(8,128)(2,1)} %refs_4_.1, ...), custom_call_target="tpu_custom_call" | custom-call | tf_op jit(solution)/shard_map/layer/pallas_call | solution.py:846
  188.7 7.9 %unpack.1 = (bf16[256,1024]{1,0:T(8,128)(2,1)}, f32[256,1024]{1,0:T(8,128)}, f32[4,1024,256]{2,1,0:T(8,128)}, f32[256,1024]{1,0:T(8,128)}, f32[2,704,1024]{2,1,0:T(8,128)}, /*index=5*/f32[704,1024]{1,0:T(8,128)}) custom-call(bf16[27136,128]{1,0:T(8,128)(2,1)} %get-tuple-element.15.flat, bf16[256,1024]{1,0:T(8,128)(2,1)} %get-tuple-element.16.lo_in, ...), custom_call_target="tpu_custom_call" | custom-call | tf_op jit(solution)/shard_map/unpack/pallas_call | solution.py:927

commit v3 on v2

--- a/solution.py
+++ b/solution.py
@@ -374,9 +374,9 @@
     low_place = lambda b, k: cot_g.at[rows(b * tb + k * hb, hb, hb), :]
     low_ag = Gather(ctx, 2, lambda k: low_place(h, k), low_place, 0)
 
-    for ag in (token_ag, cot_ag):
-        for k in range(2):
-            ag.start(k)
+    token_ag.start(0)
+    token_ag.start(1)
+    cot_ag.start(0)
 
     lane = lax.broadcasted_iota(jnp.int32, (32, HEAD_DIM), 1).astype(F32)
     step = lax.broadcasted_iota(jnp.int32, (32, HEAD_DIM), 0).astype(F32)
@@ -448,6 +448,11 @@
         for k in range(PARTS):
             gate[k, at, :] = dot(n1, r["wgate"][:, pl.ds(k * LOCAL, LOCAL)]).astype(BF)
 
+    def member(k):
+        yy = y + (k // 2) * (1 - 2 * y)
+        cc = c + lax.rem(k, 2) * (1 - 2 * c)
+        return yy * 2 + cc
+
     def project_turn(k, carry):
         @pl.when(k == 1)
         def _():
@@ -464,9 +469,7 @@
             for i in range(2):
                 token_ag.wait_relay(i)
 
-        yy = y + (k // 2) * (1 - 2 * y)
-        cc = c + lax.rem(k, 2) * (1 - 2 * c)
-        project(yy * 2 + cc)
+        project(member(k))
         return carry
 
     lax.fori_loop(0, PARTS, project_turn, 0)
@@ -493,15 +496,14 @@
     for i in range(blocks):
         attend(i)
         att_ag.start(i)
+    cot_ag.start(1)
 
     out_in.wait()
     down_in.wait()
     cot_in.wait()
     cot_ag.pass_on(0)
-    cot_ag.pass_on(1)
-    for k in range(2):
-        cot_ag.wait_beside(k)
-        cot_ag.wait_relay(k)
+    cot_ag.wait_beside(0)
+    cot_ag.wait_relay(0)
 
     def mlp(b, carry):
         for k in range(blocks):
@@ -534,11 +536,30 @@
         u = dot(n2, r["wglu"][:, pl.ds(fp, fp)])
         product = (g * u).astype(BF)
         r["product"][at, :] = product
+        dp = dot_nt(cot_g[rows(b * tb, hb, hb), :], r["wdown"][...])
+        for lanes, v in ((pl.ds(0, fp), u), (pl.ds(fp, fp), g)):
+            r["dpair"][rows(b * tb, hb, hb), lanes] = (dp * v[:hb]).astype(BF)
+            r["dpair"][rows(b * tb + hb, hb, hb), lanes] = v[hb:].astype(BF)
+        return carry
+
+    def second_half(k, carry):
+        @pl.when(k == 1)
+        def _():
+            cot_ag.wait_beside(1)
+
+        @pl.when(k == 2)
+        def _():
+            cot_ag.pass_on(1)
+
+        @pl.when(k == 3)
+        def _():
+            cot_ag.wait_relay(1)
+
+        at = rows(member(k) * tb + hb, hb, hb)
         dp = dot_nt(cot_g[at, :], r["wdown"][...])
-        dg = (dp * u).astype(BF)
-        du = (dp * g).astype(BF)
-        r["dpair"][at, pl.ds(0, fp)] = dg
-        r["dpair"][at, pl.ds(fp, fp)] = du
+        for lanes in (pl.ds(0, fp), pl.ds(fp, fp)):
+            v = r["dpair"][at, lanes].astype(F32)
+            r["dpair"][at, lanes] = (dp * v).astype(BF)
         return carry
 
     def partials(b, carry):
@@ -550,6 +571,7 @@
     token_ag.drain()
     att_ag.pass_on(0)
     lax.fori_loop(0, blocks, mlp, 0)
+    lax.fori_loop(0, PARTS, second_half, 0)
 
     dn_rs = Scatter(ctx, r["dn_part"], r["dn_near"], r["dn_cross"], 12)
     lo_rs = Scatter(ctx, r["lo_part"], r["lo_near"], r["lo_cross"], 15)

time: 197 us -> 195 us (0.990)
  Pallas kernels: 196 us -> 194 us
where the time goes in v3:
time: 195 us
  Pallas kernels  194 us (99%)
    pallas_call x1, Pallas kernels, main_call(): pl.pallas_call(kernel, name='layer', out_shape=(jax.ShapeDtypeStruct((tb,...  186 us
    pallas_call x1, Pallas kernels, unpack(): pl.pallas_call(functools.partial(unpack_kernel, sz), name='unpack', out_s...  7.88 us

profile of v3, /device:TPU:0, one launch (start us, length us, event | category | flops | bytes accessed | tf_op | source)
XLA Modules:
  0.0 195.2 jit_solution(4475895615515370762)
XLA Ops:
  0.6 186.5 %layer.1 = (bf16[256,1024]{1,0:T(8,128)(2,1)}, f32[256,1024]{1,0:T(8,128)}, bf16[27136,128]{1,0:T(8,128)(2,1)}) custom-call(bf16[256,1024]{1,0:T(8,128)(2,1)} %refs_0_.1, bf16[4,1024,1024]{2,1,0:T(8,128)(2,1)} %refs_1_.1, bf16[1024,1024]{1,0:T(8,128)(2,1)} %refs_2_.1, bf16[2,1024,2816]{2,1,0:T(8,128)(2,1)} %refs_3_.1, bf16[2816,1024]{1,0:T(8,128)(2,1)} %refs_4_.1, ...), custom_call_target="tpu_custom_call" | custom-call | tf_op jit(solution)/shard_map/layer/pallas_call | solution.py:868
  187.1 7.9 %unpack.1 = (bf16[256,1024]{1,0:T(8,128)(2,1)}, f32[256,1024]{1,0:T(8,128)}, f32[4,1024,256]{2,1,0:T(8,128)}, f32[256,1024]{1,0:T(8,128)}, f32[2,704,1024]{2,1,0:T(8,128)}, /*index=5*/f32[704,1024]{1,0:T(8,128)}) custom-call(bf16[27136,128]{1,0:T(8,128)(2,1)} %get-tuple-element.15.flat, bf16[256,1024]{1,0:T(8,128)(2,1)} %get-tuple-element.16.lo_in, ...), custom_call_target="tpu_custom_call" | custom-call | tf_op jit(solution)/shard_map/unpack/pallas_call | solution.py:949

commit v4 on v3

--- a/solution.py
+++ b/solution.py
@@ -354,6 +354,8 @@
     pl.semaphore_wait(barrier, 4)
 
     hb = tb // 2
+    late = tb // 4
+    early = tb - late
     token_ag = Gather(
         ctx,
         2,
@@ -364,8 +366,8 @@
     cot_ag = Gather(
         ctx,
         2,
-        lambda k: cot.at[pl.ds(k * hb, hb), :],
-        lambda b, k: cot_g.at[rows(b * tb + k * hb, hb, hb), :],
+        lambda k: cot.at[pl.ds(k * early, (tb - early) if k else early), :],
+        lambda b, k: cot_g.at[rows(b * tb + k * early, (tb - early) if k else early, late), :],
         6,
     )
     blocks = t_all // 256
@@ -536,10 +538,10 @@
         u = dot(n2, r["wglu"][:, pl.ds(fp, fp)])
         product = (g * u).astype(BF)
         r["product"][at, :] = product
-        dp = dot_nt(cot_g[rows(b * tb, hb, hb), :], r["wdown"][...])
+        dp = dot_nt(cot_g[rows(b * tb, early, late), :], r["wdown"][...])
         for lanes, v in ((pl.ds(0, fp), u), (pl.ds(fp, fp), g)):
-            r["dpair"][rows(b * tb, hb, hb), lanes] = (dp * v[:hb]).astype(BF)
-            r["dpair"][rows(b * tb + hb, hb, hb), lanes] = v[hb:].astype(BF)
+            r["dpair"][rows(b * tb, early, late), lanes] = (dp * v[:early]).astype(BF)
+            r["dpair"][rows(b * tb + early, late, late), lanes] = v[early:].astype(BF)
         return carry
 
     def second_half(k, carry):
@@ -555,7 +557,7 @@
         def _():
             cot_ag.wait_relay(1)
 
-        at = rows(member(k) * tb + hb, hb, hb)
+        at = rows(member(k) * tb + early, late, late)
         dp = dot_nt(cot_g[at, :], r["wdown"][...])
         for lanes in (pl.ds(0, fp), pl.ds(fp, fp)):
             v = r["dpair"][at, lanes].astype(F32)

time: 195 us -> 198 us (1.015)
  Pallas kernels: 194 us -> 197 us
    pallas_call x1, Pallas kernels: 186 us -> 189 us  [main_call(): pl.pallas_call(kernel, name='layer', out_shape=(jax.ShapeDtypeStruct((tb,...]
where the time goes in v4:
time: 198 us
  Pallas kernels  197 us (99%)
    pallas_call x1, Pallas kernels, main_call(): pl.pallas_call(kernel, name='layer', out_shape=(jax.ShapeDtypeStruct((tb,...  189 us
    pallas_call x1, Pallas kernels, unpack(): pl.pallas_call(functools.partial(unpack_kernel, sz), name='unpack', out_s...  7.88 us

profile of v4, /device:TPU:0, one launch (start us, length us, event | category | flops | bytes accessed | tf_op | source)
XLA Modules:
  0.0 197.9 jit_solution(15029951484436787733)
XLA Ops:
  0.6 189.2 %layer.1 = (bf16[256,1024]{1,0:T(8,128)(2,1)}, f32[256,1024]{1,0:T(8,128)}, bf16[27136,128]{1,0:T(8,128)(2,1)}) custom-call(bf16[256,1024]{1,0:T(8,128)(2,1)} %refs_0_.1, bf16[4,1024,1024]{2,1,0:T(8,128)(2,1)} %refs_1_.1, bf16[1024,1024]{1,0:T(8,128)(2,1)} %refs_2_.1, bf16[2,1024,2816]{2,1,0:T(8,128)(2,1)} %refs_3_.1, bf16[2816,1024]{1,0:T(8,128)(2,1)} %refs_4_.1, ...), custom_call_target="tpu_custom_call" | custom-call | tf_op jit(solution)/shard_map/layer/pallas_call | solution.py:870
  189.9 7.9 %unpack.1 = (bf16[256,1024]{1,0:T(8,128)(2,1)}, f32[256,1024]{1,0:T(8,128)}, f32[4,1024,256]{2,1,0:T(8,128)}, f32[256,1024]{1,0:T(8,128)}, f32[2,704,1024]{2,1,0:T(8,128)}, /*index=5*/f32[704,1024]{1,0:T(8,128)}) custom-call(bf16[27136,128]{1,0:T(8,128)(2,1)} %get-tuple-element.15.flat, bf16[256,1024]{1,0:T(8,128)(2,1)} %get-tuple-element.16.lo_in, ...), custom_call_target="tpu_custom_call" | custom-call | tf_op jit(solution)/shard_map/unpack/pallas_call | solution.py:951
